TPU v7x, 16 devices: a 4x2x1 block of a 4x4x8 slice. The times are simulated.
16 devices in a mesh: dp: 2 (over y, z), cp: 8 (over x, core).
Axes of the slice: x: 4, y: 2, z: 1, core: 2. Of those that a mesh axis runs over, the one named last changes fastest.
The devices are a block of a 4x4x8 slice.
Arguments:
- hidden: bfloat16 [16, 1024, 896], P('dp', 'cp'), parts along dimension 0
- positions: int32 [16, 1024], P('dp', 'cp'), parts along dimension 0
- norm_gain: bfloat16 [896], replicated
- w_query: bfloat16 [896, 896], replicated
- w_key: bfloat16 [896, 128], replicated
- w_value: bfloat16 [896, 128], replicated
- w_out: bfloat16 [14, 64, 896], replicated
Outputs:
- output: bfloat16 [16, 1024, 896], P('dp', 'cp'), parts along dimension 0
There are 2 independent parts. A program takes and returns all parts, laid end to end along the dimension named above; an argument that names none is the same for every part.
All inputs are finite; a program needn't handle non-finite values.
Results may differ from a plain program's by a relative error of at most 0.00739962.
Values are sent between devices in bfloat16 or wider.
A program may use at most 768 MiB of HBM per device.

v0:
```python
import jax
import jax.numpy as jnp
from jax import lax
from jax.sharding import PartitionSpec as P


def rms_norm(hidden, norm_gain):
    x_f32 = hidden.astype(jnp.float32)
    inv_rms = lax.rsqrt(jnp.mean(x_f32 * x_f32, axis=-1, keepdims=True) + 1e-5)
    return (x_f32 * inv_rms * norm_gain.astype(jnp.float32)).astype(jnp.bfloat16)


def rotary(proj_f32, positions):
    head_dim = proj_f32.shape[-1]
    half_dim = head_dim // 2
    inv_freq = 10000.0 ** (-2.0 * jnp.arange(half_dim, dtype=jnp.float32) / head_dim)
    angles = positions.astype(jnp.float32)[:, :, None] * inv_freq
    cos_part = jnp.cos(angles)[:, :, None, :]
    sin_part = jnp.sin(angles)[:, :, None, :]
    first_half = proj_f32[..., :half_dim]
    second_half = proj_f32[..., half_dim:]
    return jnp.concatenate([first_half * cos_part - second_half * sin_part, second_half * cos_part + first_half * sin_part], axis=-1).astype(jnp.bfloat16)


def attend_block(q_grp, k_blk, v_blk, att_state, allowed):
    run_max, run_sum, acc_out = att_state
    scores = jnp.einsum('bqkgd,bskd->bkgqs', q_grp, k_blk, preferred_element_type=jnp.float32) * (q_grp.shape[-1] ** -0.5)
    if allowed is not None:
        scores = jnp.where(allowed, scores, -jnp.inf)
    new_max = jnp.maximum(run_max, jnp.max(scores, axis=-1))
    prob_blk = jnp.exp(scores - new_max[..., None])
    rescale = jnp.exp(run_max - new_max)
    new_sum = run_sum * rescale + jnp.sum(prob_blk, axis=-1)
    new_acc = acc_out * rescale[..., None] + jnp.einsum('bkgqs,bskd->bkgqd', prob_blk, v_blk, preferred_element_type=jnp.float32)
    return new_max, new_sum, new_acc


def solution(mesh):
    n_cp = mesh.shape['cp']
    shift_pairs = [(src_dev, (src_dev + 1) % n_cp) for src_dev in range(n_cp)]

    def local_block(hidden, positions, norm_gain, w_query, w_key, w_value, w_out):
        batch_loc, seq_loc, model_dim = hidden.shape
        n_heads, head_dim, _ = w_out.shape
        n_kv = w_key.shape[1] // head_dim
        n_groups = n_heads // n_kv
        normed = rms_norm(hidden, norm_gain)
        q_rot = rotary(jnp.einsum('bsd,de->bse', normed, w_query, preferred_element_type=jnp.float32).reshape(batch_loc, seq_loc, n_heads, head_dim), positions)
        k_rot = rotary(jnp.einsum('bsd,de->bse', normed, w_key, preferred_element_type=jnp.float32).reshape(batch_loc, seq_loc, n_kv, head_dim), positions)
        v_loc = jnp.einsum('bsd,de->bse', normed, w_value, preferred_element_type=jnp.float32).astype(jnp.bfloat16).reshape(batch_loc, seq_loc, n_kv, head_dim)
        q_grp = q_rot.reshape(batch_loc, seq_loc, n_kv, n_groups, head_dim)
        my_index = lax.axis_index('cp')
        token_idx = jnp.arange(seq_loc)
        diag_mask = token_idx[:, None] >= token_idx[None, :]
        start_state = (
            jnp.full((batch_loc, n_kv, n_groups, seq_loc), -jnp.inf, jnp.float32),
            jnp.zeros((batch_loc, n_kv, n_groups, seq_loc), jnp.float32),
            jnp.zeros((batch_loc, n_kv, n_groups, seq_loc, head_dim), jnp.float32),
        )
        att_state = attend_block(q_grp, k_rot, v_loc, start_state, diag_mask)

        def step_fn(step_idx, loop_state):
            k_blk, v_blk, att_prev = loop_state
            k_blk, v_blk = lax.ppermute((k_blk, v_blk), 'cp', shift_pairs)
            src_block = (my_index - step_idx) % n_cp
            att_next = lax.cond(src_block < my_index, lambda state_kept: attend_block(q_grp, k_blk, v_blk, state_kept, None), lambda state_kept: state_kept, att_prev)
            return k_blk, v_blk, att_next

        _, _, final_state = lax.fori_loop(1, n_cp, step_fn, (k_rot, v_loc, att_state))
        run_max, run_sum, acc_out = final_state
        attn_out = (acc_out / run_sum[..., None]).astype(jnp.bfloat16)
        proj_out = jnp.einsum('bkgqd,kgde->bqe', attn_out, w_out.reshape(n_kv, n_groups, head_dim, model_dim), preferred_element_type=jnp.float32)
        return (hidden.astype(jnp.float32) + proj_out).astype(jnp.bfloat16)

    act_spec = P('dp', 'cp', None)
    return jax.shard_map(local_block, mesh=mesh, in_specs=(act_spec, P('dp', 'cp'), P(), P(), P(), P(), P()), out_specs=act_spec, check_vma=False)
```

profile of v0, /device:TPU:119, one launch (start us, length us, event | category | flops | bytes accessed | tf_op | source)
XLA Modules:
  0.0 171.0 jit_solution(8024919258477695813)
XLA Ops:
  2.8 4.2 %fusion.25 = f32[8,128,896]{1,2,0:T(8,128)S(1)} fusion(bf16[896,896]{1,0:T(8,128)(2,1)} %param.14, bf16[8,128,896]{2,1,0:T(8,128)(2,1)} %param.11, f32[896]{0:T(1024)S(1)} %convert_element_type.37, f32[8,128]{1,0:T(8,128)S(1)} %add_rsqrt_fusion), kind=kOutput, calls=%fused_computation.36 | convolution fusion | flops 1647837184 | bytes 7118336 | tf_op jit(solution)/shard_map/bsd,de->bse/dot_general | solution.py:48
  10.7 2.3 %fusion.13 = f32[8,2,7,128]{3,2,1,0:T(8,128)S(1)} fusion(f32[8,2,128,128,7]{3,2,4,1,0:T(8,128)S(1)} %get-tuple-element.278, f32[8,2,7,128]{3,2,1,0:T(8,128)S(1)} %get-tuple-element.343, pred[128,128]{0,1:T(8,128)(4,1)S(1)} %iota_compare_fusion), kind=kLoop, calls=%fused_computation.17 | loop fusion | flops 7325696 | bytes 7471104 | tf_op jit(solution)/shard_map/reduce_sum | solution.py:33
  14.4 3.4 %fusion.23 = f32[8,2,7,128,64]{3,4,2,1,0:T(8,128)} fusion(bf16[8,128,2,64,1]{1,3,4,2,0:T(8,128)(2,1)S(1)} %bitcast.81, f32[8,2,128,128,7]{3,2,4,1,0:T(8,128)S(1)} %get-tuple-element.278, f32[8,2,7,128]{3,2,1,0:T(8,128)S(1)} %get-tuple-element.343, pred[128,128]{0,1:T(8,128)(4,1)S(1)} %iota_compare_fusion, f32[8,2,7,128]{3,2,1,0:T(8,128)S(1)} %get-tuple-element.273), kind=kOutput, calls=%fused_computation.31 | convolution fusion | flops 241303552 | bytes 11403264 | tf_op jit(solution)/shard_map/bkgqs,bskd->bkgqd/dot_general | solution.py:34
  18.8 146.0 %while.23 = (s32[]{:T(128)}, bf16[8,128,2,64]{1,3,2,0:T(8,128)(2,1)}, bf16[8,128,2,64]{1,3,2,0:T(8,128)(2,1)}, f32[8,2,7,128]{3,2,1,0:T(8,128)S(1)}, f32[8,2,7,1...) while((s32[]{:T(128)}, ...), condition=%wide.region_8.9_spmd, body=%wide.region_3.8_spmd.sunk | while | flops 484470784 | bytes 65602084 | solution.py:69
  18.8 3.3 %collective-permute-done = bf16[8,128,2,64]{1,3,2,0:T(8,128)(2,1)} collective-permute-done((bf16[8,128,2,64]{1,3,2,0:T(8,128)(2,1)}, bf16[8,128,2,64]{1,3,2,0:T(8,128)(2,1)}, u32[]{:S(2)}, u32[]{:S(2)}) %collective-permute-start) | collective-permute-done | bytes 262176 | tf_op jit(solution)/shard_map/while/body/eval_jaxpr/ppermute | solution.py:64
  22.1 2.8 %collective-permute-done.1 = bf16[8,128,2,64]{1,3,2,0:T(8,128)(2,1)} collective-permute-done((bf16[8,128,2,64]{1,3,2,0:T(8,128)(2,1)}, bf16[8,128,2,64]{1,3,2,0:T(8,128)(2,1)}, u32[]{:S(2)}, u32[]{:S(2)}) %collective-permute-start.1) | collective-permute-done | bytes 262176 | tf_op jit(solution)/shard_map/while/body/eval_jaxpr/ppermute | solution.py:64
  24.9 9.9 %conditional.2 = ((f32[8,2,7,128]{3,2,1,0:T(8,128)S(1)}, f32[8,2,7,128]{3,2,1,0:T(8,128)}, f32[8,2,7,128,64]{3,4,2,1,0:T(8,128)})) conditional(s32[]{:T(128)} %convert_element_type.66, (f32[8,2,7,128]{3,2,1,0:T(8,128)S(1)}, f32[8,2,7,128]{3,2,1,0:T(8,128)}, f32[8,2,7,128,64]{3,4,2,1,0:T(8,128)}) %tuple.52, (bf16[8,128,2,64]{1,3,2,0:T(8,128)(2,1)}, ...), branch_computations={%region_4.4_spmd, %region_5.7_spmd} | conditional | flops 484470784 | bytes 62455952 | solution.py:66
  29.8 3.2 %multiply_add_fusion = f32[8,2,7,128,64]{3,4,2,1,0:T(8,128)S(1)} fusion(f32[8,2,7,128,64]{3,4,2,1,0:T(8,128)S(1)} %copy-done.1, f32[8,2,128,128,7]{3,2,4,1,0:T(8,128)S(1)} %get-tuple-element.268, f32[8,2,7,128]{3,2,1,0:T(8,128)S(1)} %max.2, f32[8,2,7,128]{3,2,1,0:T(8,128)S(1)} %get-tuple-element.266, bf16[8,128,2,64]{1,3,2,0:T(8,128)(2,1)} %get-tuple-element.232), kind=kOutput, calls=%fused_computation.5 | convolution fusion | flops 240386048 | bytes 15056896 | tf_op jit(solution)/shard_map/while/body/eval_jaxpr/cond/branch_1_fun/bkgqs,bskd->bkgqd/dot_general | solution.py:34
  44.2 9.9 %conditional.2 = ((f32[8,2,7,128]{3,2,1,0:T(8,128)S(1)}, f32[8,2,7,128]{3,2,1,0:T(8,128)}, f32[8,2,7,128,64]{3,4,2,1,0:T(8,128)})) conditional(s32[]{:T(128)} %convert_element_type.66, (f32[8,2,7,128]{3,2,1,0:T(8,128)S(1)}, f32[8,2,7,128]{3,2,1,0:T(8,128)}, f32[8,2,7,128,64]{3,4,2,1,0:T(8,128)}) %tuple.52, (bf16[8,128,2,64]{1,3,2,0:T(8,128)(2,1)}, ...), branch_computations={%region_4.4_spmd, %region_5.7_spmd} | conditional | flops 484470784 | bytes 62455952 | solution.py:66
  44.2 2.1 %bitcast_reduce_fusion = (f32[8,2,7,128]{3,2,1,0:T(8,128)S(1)}, f32[8,2,128,128,7]{3,2,4,1,0:T(8,128)S(1)}) fusion(bf16[8,128,2,7,64]{1,4,3,2,0:T(8,128)(2,1)S(1)} %get-tuple-element.229, bf16[8,128,2,64]{1,3,2,0:T(8,128)(2,1)} %get-tuple-element.228), kind=kOutput, calls=%fused_computation.1 | convolution fusion | flops 238536704 | bytes 9494528 | tf_op jit(solution)/shard_map/while/body/eval_jaxpr/cond/branch_1_fun/bqkgd,bskd->bkgqs/dot_general | solution.py:27
  49.1 3.2 %multiply_add_fusion = f32[8,2,7,128,64]{3,4,2,1,0:T(8,128)S(1)} fusion(f32[8,2,7,128,64]{3,4,2,1,0:T(8,128)S(1)} %copy-done.1, f32[8,2,128,128,7]{3,2,4,1,0:T(8,128)S(1)} %get-tuple-element.268, f32[8,2,7,128]{3,2,1,0:T(8,128)S(1)} %max.2, f32[8,2,7,128]{3,2,1,0:T(8,128)S(1)} %get-tuple-element.266, bf16[8,128,2,64]{1,3,2,0:T(8,128)(2,1)} %get-tuple-element.232), kind=kOutput, calls=%fused_computation.5 | convolution fusion | flops 240386048 | bytes 15056896 | tf_op jit(solution)/shard_map/while/body/eval_jaxpr/cond/branch_1_fun/bkgqs,bskd->bkgqd/dot_general | solution.py:34
  57.4 6.6 %collective-permute-done = bf16[8,128,2,64]{1,3,2,0:T(8,128)(2,1)} collective-permute-done((bf16[8,128,2,64]{1,3,2,0:T(8,128)(2,1)}, bf16[8,128,2,64]{1,3,2,0:T(8,128)(2,1)}, u32[]{:S(2)}, u32[]{:S(2)}) %collective-permute-start) | collective-permute-done | bytes 262176 | tf_op jit(solution)/shard_map/while/body/eval_jaxpr/ppermute | solution.py:64
  64.4 9.9 %conditional.2 = ((f32[8,2,7,128]{3,2,1,0:T(8,128)S(1)}, f32[8,2,7,128]{3,2,1,0:T(8,128)}, f32[8,2,7,128,64]{3,4,2,1,0:T(8,128)})) conditional(s32[]{:T(128)} %convert_element_type.66, (f32[8,2,7,128]{3,2,1,0:T(8,128)S(1)}, f32[8,2,7,128]{3,2,1,0:T(8,128)}, f32[8,2,7,128,64]{3,4,2,1,0:T(8,128)}) %tuple.52, (bf16[8,128,2,64]{1,3,2,0:T(8,128)(2,1)}, ...), branch_computations={%region_4.4_spmd, %region_5.7_spmd} | conditional | flops 484470784 | bytes 62455952 | solution.py:66
  64.4 2.1 %bitcast_reduce_fusion = (f32[8,2,7,128]{3,2,1,0:T(8,128)S(1)}, f32[8,2,128,128,7]{3,2,4,1,0:T(8,128)S(1)}) fusion(bf16[8,128,2,7,64]{1,4,3,2,0:T(8,128)(2,1)S(1)} %get-tuple-element.229, bf16[8,128,2,64]{1,3,2,0:T(8,128)(2,1)} %get-tuple-element.228), kind=kOutput, calls=%fused_computation.1 | convolution fusion | flops 238536704 | bytes 9494528 | tf_op jit(solution)/shard_map/while/body/eval_jaxpr/cond/branch_1_fun/bqkgd,bskd->bkgqs/dot_general | solution.py:27
  69.2 3.2 %multiply_add_fusion = f32[8,2,7,128,64]{3,4,2,1,0:T(8,128)S(1)} fusion(f32[8,2,7,128,64]{3,4,2,1,0:T(8,128)S(1)} %copy-done.1, f32[8,2,128,128,7]{3,2,4,1,0:T(8,128)S(1)} %get-tuple-element.268, f32[8,2,7,128]{3,2,1,0:T(8,128)S(1)} %max.2, f32[8,2,7,128]{3,2,1,0:T(8,128)S(1)} %get-tuple-element.266, bf16[8,128,2,64]{1,3,2,0:T(8,128)(2,1)} %get-tuple-element.232), kind=kOutput, calls=%fused_computation.5 | convolution fusion | flops 240386048 | bytes 15056896 | tf_op jit(solution)/shard_map/while/body/eval_jaxpr/cond/branch_1_fun/bkgqs,bskd->bkgqd/dot_general | solution.py:34
  77.6 8.2 %collective-permute-done = bf16[8,128,2,64]{1,3,2,0:T(8,128)(2,1)} collective-permute-done((bf16[8,128,2,64]{1,3,2,0:T(8,128)(2,1)}, bf16[8,128,2,64]{1,3,2,0:T(8,128)(2,1)}, u32[]{:S(2)}, u32[]{:S(2)}) %collective-permute-start) | collective-permute-done | bytes 262176 | tf_op jit(solution)/shard_map/while/body/eval_jaxpr/ppermute | solution.py:64
  86.2 9.9 %conditional.2 = ((f32[8,2,7,128]{3,2,1,0:T(8,128)S(1)}, f32[8,2,7,128]{3,2,1,0:T(8,128)}, f32[8,2,7,128,64]{3,4,2,1,0:T(8,128)})) conditional(s32[]{:T(128)} %convert_element_type.66, (f32[8,2,7,128]{3,2,1,0:T(8,128)S(1)}, f32[8,2,7,128]{3,2,1,0:T(8,128)}, f32[8,2,7,128,64]{3,4,2,1,0:T(8,128)}) %tuple.52, (bf16[8,128,2,64]{1,3,2,0:T(8,128)(2,1)}, ...), branch_computations={%region_4.4_spmd, %region_5.7_spmd} | conditional | flops 484470784 | bytes 62455952 | solution.py:66
  86.2 2.1 %bitcast_reduce_fusion = (f32[8,2,7,128]{3,2,1,0:T(8,128)S(1)}, f32[8,2,128,128,7]{3,2,4,1,0:T(8,128)S(1)}) fusion(bf16[8,128,2,7,64]{1,4,3,2,0:T(8,128)(2,1)S(1)} %get-tuple-element.229, bf16[8,128,2,64]{1,3,2,0:T(8,128)(2,1)} %get-tuple-element.228), kind=kOutput, calls=%fused_computation.1 | convolution fusion | flops 238536704 | bytes 9494528 | tf_op jit(solution)/shard_map/while/body/eval_jaxpr/cond/branch_1_fun/bqkgd,bskd->bkgqs/dot_general | solution.py:27
  91.0 3.2 %multiply_add_fusion = f32[8,2,7,128,64]{3,4,2,1,0:T(8,128)S(1)} fusion(f32[8,2,7,128,64]{3,4,2,1,0:T(8,128)S(1)} %copy-done.1, f32[8,2,128,128,7]{3,2,4,1,0:T(8,128)S(1)} %get-tuple-element.268, f32[8,2,7,128]{3,2,1,0:T(8,128)S(1)} %max.2, f32[8,2,7,128]{3,2,1,0:T(8,128)S(1)} %get-tuple-element.266, bf16[8,128,2,64]{1,3,2,0:T(8,128)(2,1)} %get-tuple-element.232), kind=kOutput, calls=%fused_computation.5 | convolution fusion | flops 240386048 | bytes 15056896 | tf_op jit(solution)/shard_map/while/body/eval_jaxpr/cond/branch_1_fun/bkgqs,bskd->bkgqd/dot_general | solution.py:34
  99.4 8.2 %collective-permute-done = bf16[8,128,2,64]{1,3,2,0:T(8,128)(2,1)} collective-permute-done((bf16[8,128,2,64]{1,3,2,0:T(8,128)(2,1)}, bf16[8,128,2,64]{1,3,2,0:T(8,128)(2,1)}, u32[]{:S(2)}, u32[]{:S(2)}) %collective-permute-start) | collective-permute-done | bytes 262176 | tf_op jit(solution)/shard_map/while/body/eval_jaxpr/ppermute | solution.py:64
  108.0 9.9 %conditional.2 = ((f32[8,2,7,128]{3,2,1,0:T(8,128)S(1)}, f32[8,2,7,128]{3,2,1,0:T(8,128)}, f32[8,2,7,128,64]{3,4,2,1,0:T(8,128)})) conditional(s32[]{:T(128)} %convert_element_type.66, (f32[8,2,7,128]{3,2,1,0:T(8,128)S(1)}, f32[8,2,7,128]{3,2,1,0:T(8,128)}, f32[8,2,7,128,64]{3,4,2,1,0:T(8,128)}) %tuple.52, (bf16[8,128,2,64]{1,3,2,0:T(8,128)(2,1)}, ...), branch_computations={%region_4.4_spmd, %region_5.7_spmd} | conditional | flops 484470784 | bytes 62455952 | solution.py:66
  108.0 2.1 %bitcast_reduce_fusion = (f32[8,2,7,128]{3,2,1,0:T(8,128)S(1)}, f32[8,2,128,128,7]{3,2,4,1,0:T(8,128)S(1)}) fusion(bf16[8,128,2,7,64]{1,4,3,2,0:T(8,128)(2,1)S(1)} %get-tuple-element.229, bf16[8,128,2,64]{1,3,2,0:T(8,128)(2,1)} %get-tuple-element.228), kind=kOutput, calls=%fused_computation.1 | convolution fusion | flops 238536704 | bytes 9494528 | tf_op jit(solution)/shard_map/while/body/eval_jaxpr/cond/branch_1_fun/bqkgd,bskd->bkgqs/dot_general | solution.py:27
  112.9 3.2 %multiply_add_fusion = f32[8,2,7,128,64]{3,4,2,1,0:T(8,128)S(1)} fusion(f32[8,2,7,128,64]{3,4,2,1,0:T(8,128)S(1)} %copy-done.1, f32[8,2,128,128,7]{3,2,4,1,0:T(8,128)S(1)} %get-tuple-element.268, f32[8,2,7,128]{3,2,1,0:T(8,128)S(1)} %max.2, f32[8,2,7,128]{3,2,1,0:T(8,128)S(1)} %get-tuple-element.266, bf16[8,128,2,64]{1,3,2,0:T(8,128)(2,1)} %get-tuple-element.232), kind=kOutput, calls=%fused_computation.5 | convolution fusion | flops 240386048 | bytes 15056896 | tf_op jit(solution)/shard_map/while/body/eval_jaxpr/cond/branch_1_fun/bkgqs,bskd->bkgqd/dot_general | solution.py:34
  121.2 8.2 %collective-permute-done = bf16[8,128,2,64]{1,3,2,0:T(8,128)(2,1)} collective-permute-done((bf16[8,128,2,64]{1,3,2,0:T(8,128)(2,1)}, bf16[8,128,2,64]{1,3,2,0:T(8,128)(2,1)}, u32[]{:S(2)}, u32[]{:S(2)}) %collective-permute-start) | collective-permute-done | bytes 262176 | tf_op jit(solution)/shard_map/while/body/eval_jaxpr/ppermute | solution.py:64
  129.8 9.9 %conditional.2 = ((f32[8,2,7,128]{3,2,1,0:T(8,128)S(1)}, f32[8,2,7,128]{3,2,1,0:T(8,128)}, f32[8,2,7,128,64]{3,4,2,1,0:T(8,128)})) conditional(s32[]{:T(128)} %convert_element_type.66, (f32[8,2,7,128]{3,2,1,0:T(8,128)S(1)}, f32[8,2,7,128]{3,2,1,0:T(8,128)}, f32[8,2,7,128,64]{3,4,2,1,0:T(8,128)}) %tuple.52, (bf16[8,128,2,64]{1,3,2,0:T(8,128)(2,1)}, ...), branch_computations={%region_4.4_spmd, %region_5.7_spmd} | conditional | flops 484470784 | bytes 62455952 | solution.py:66
  129.8 2.1 %bitcast_reduce_fusion = (f32[8,2,7,128]{3,2,1,0:T(8,128)S(1)}, f32[8,2,128,128,7]{3,2,4,1,0:T(8,128)S(1)}) fusion(bf16[8,128,2,7,64]{1,4,3,2,0:T(8,128)(2,1)S(1)} %get-tuple-element.229, bf16[8,128,2,64]{1,3,2,0:T(8,128)(2,1)} %get-tuple-element.228), kind=kOutput, calls=%fused_computation.1 | convolution fusion | flops 238536704 | bytes 9494528 | tf_op jit(solution)/shard_map/while/body/eval_jaxpr/cond/branch_1_fun/bqkgd,bskd->bkgqs/dot_general | solution.py:27
  134.7 3.2 %multiply_add_fusion = f32[8,2,7,128,64]{3,4,2,1,0:T(8,128)S(1)} fusion(f32[8,2,7,128,64]{3,4,2,1,0:T(8,128)S(1)} %copy-done.1, f32[8,2,128,128,7]{3,2,4,1,0:T(8,128)S(1)} %get-tuple-element.268, f32[8,2,7,128]{3,2,1,0:T(8,128)S(1)} %max.2, f32[8,2,7,128]{3,2,1,0:T(8,128)S(1)} %get-tuple-element.266, bf16[8,128,2,64]{1,3,2,0:T(8,128)(2,1)} %get-tuple-element.232), kind=kOutput, calls=%fused_computation.5 | convolution fusion | flops 240386048 | bytes 15056896 | tf_op jit(solution)/shard_map/while/body/eval_jaxpr/cond/branch_1_fun/bkgqs,bskd->bkgqd/dot_general | solution.py:34
  143.0 8.2 %collective-permute-done = bf16[8,128,2,64]{1,3,2,0:T(8,128)(2,1)} collective-permute-done((bf16[8,128,2,64]{1,3,2,0:T(8,128)(2,1)}, bf16[8,128,2,64]{1,3,2,0:T(8,128)(2,1)}, u32[]{:S(2)}, u32[]{:S(2)}) %collective-permute-start) | collective-permute-done | bytes 262176 | tf_op jit(solution)/shard_map/while/body/eval_jaxpr/ppermute | solution.py:64
  151.6 9.9 %conditional.2 = ((f32[8,2,7,128]{3,2,1,0:T(8,128)S(1)}, f32[8,2,7,128]{3,2,1,0:T(8,128)}, f32[8,2,7,128,64]{3,4,2,1,0:T(8,128)})) conditional(s32[]{:T(128)} %convert_element_type.66, (f32[8,2,7,128]{3,2,1,0:T(8,128)S(1)}, f32[8,2,7,128]{3,2,1,0:T(8,128)}, f32[8,2,7,128,64]{3,4,2,1,0:T(8,128)}) %tuple.52, (bf16[8,128,2,64]{1,3,2,0:T(8,128)(2,1)}, ...), branch_computations={%region_4.4_spmd, %region_5.7_spmd} | conditional | flops 484470784 | bytes 62455952 | solution.py:66
  151.6 2.1 %bitcast_reduce_fusion = (f32[8,2,7,128]{3,2,1,0:T(8,128)S(1)}, f32[8,2,128,128,7]{3,2,4,1,0:T(8,128)S(1)}) fusion(bf16[8,128,2,7,64]{1,4,3,2,0:T(8,128)(2,1)S(1)} %get-tuple-element.229, bf16[8,128,2,64]{1,3,2,0:T(8,128)(2,1)} %get-tuple-element.228), kind=kOutput, calls=%fused_computation.1 | convolution fusion | flops 238536704 | bytes 9494528 | tf_op jit(solution)/shard_map/while/body/eval_jaxpr/cond/branch_1_fun/bqkgd,bskd->bkgqs/dot_general | solution.py:27
  156.5 3.2 %multiply_add_fusion = f32[8,2,7,128,64]{3,4,2,1,0:T(8,128)S(1)} fusion(f32[8,2,7,128,64]{3,4,2,1,0:T(8,128)S(1)} %copy-done.1, f32[8,2,128,128,7]{3,2,4,1,0:T(8,128)S(1)} %get-tuple-element.268, f32[8,2,7,128]{3,2,1,0:T(8,128)S(1)} %max.2, f32[8,2,7,128]{3,2,1,0:T(8,128)S(1)} %get-tuple-element.266, bf16[8,128,2,64]{1,3,2,0:T(8,128)(2,1)} %get-tuple-element.232), kind=kOutput, calls=%fused_computation.5 | convolution fusion | flops 240386048 | bytes 15056896 | tf_op jit(solution)/shard_map/while/body/eval_jaxpr/cond/branch_1_fun/bkgqs,bskd->bkgqd/dot_general | solution.py:34
  164.8 6.2 %fusion.18 = bf16[8,128,896]{2,1,0:T(8,128)(2,1)} fusion(bf16[8,128,896]{2,1,0:T(8,128)(2,1)} %param.11, bf16[2,7,64,896,1]{3,2,1,0,4:T(8,128)(2,1)S(1)} %bitcast.74, f32[8,2,7,128,64]{3,4,2,1,0:T(8,128)} %get-tuple-element.247, f32[8,2,7,128]{3,2,1,0:T(8,128)} %get-tuple-element.248), kind=kOutput, calls=%fused_computation.25 | convolution fusion | flops 1648754688 | bytes 9003008 | tf_op jit(solution)/shard_map/bkgqd,kgde->bqe/dot_general | solution.py:72
  (147 shorter events, 73.4 us)
Async XLA Ops:
  0.0 164.8 %copy-start = (bf16[14,64,896]{2,1,0:T(8,128)(2,1)S(1)}, bf16[14,64,896]{2,1,0:T(8,128)(2,1)}, u32[]{:S(2)}) copy-start(bf16[14,64,896]{2,1,0:T(8,128)(2,1)} %param.17) | copy-start | bytes 4816900
  2.7 4.3 %copy-start.7 = (s32[8,128]{1,0:T(8,128)S(1)}, s32[8,128]{1,0:T(8,128)}, u32[]{:S(2)}) copy-start(s32[8,128]{1,0:T(8,128)} %param.12) | copy-start | bytes 12292
  10.6 3.0 %copy-start.9 = (bf16[896,128]{1,0:T(8,128)(2,1)S(1)}, bf16[896,128]{1,0:T(8,128)(2,1)}, u32[]{:S(2)}) copy-start(bf16[896,128]{1,0:T(8,128)(2,1)} %param.16) | copy-start | bytes 688132
  14.4 3.4 %copy-start.6 = (bf16[8,128,128]{1,2,0:T(8,128)(2,1)}, bf16[8,128,128]{1,2,0:T(8,128)(2,1)S(1)}, u32[]{:S(2)}) copy-start(bf16[8,128,128]{1,2,0:T(8,128)(2,1)S(1)} %convolution_convert_fusion) | copy-start | bytes 786436
  18.8 3.3 %collective-permute-start = (bf16[8,128,2,64]{1,3,2,0:T(8,128)(2,1)}, bf16[8,128,2,64]{1,3,2,0:T(8,128)(2,1)}, u32[]{:S(2)}, u32[]{:S(2)}) collective-permute-start(bf16[8,128,2,64]{1,3,2,0:T(8,128)(2,1)} %get-tuple-element.353), channel_id=1, source_target_pairs={{0,1},{1,2},{2,3},{3,4},{4,5},{5,6},{6,7},{7,0},{8,9},{9,10},{10,1... | collective-permute-start | bytes 786440 | tf_op jit(solution)/shard_map/while/body/eval_jaxpr/ppermute | solution.py:64
  18.8 6.1 %collective-permute-start.1 = (bf16[8,128,2,64]{1,3,2,0:T(8,128)(2,1)}, bf16[8,128,2,64]{1,3,2,0:T(8,128)(2,1)}, u32[]{:S(2)}, u32[]{:S(2)}) collective-permute-start(bf16[8,128,2,64]{1,3,2,0:T(8,128)(2,1)} %get-tuple-element.354), channel_id=1, source_target_pairs={{0,1},{1,2},{2,3},{3,4},{4,5},{5,6},{6,7},{7,0},{8,9},{9,10},{10,1... | collective-permute-start | bytes 786440 | tf_op jit(solution)/shard_map/while/body/eval_jaxpr/ppermute | solution.py:64
  27.1 2.0 %copy-start.3 = (f32[8,2,7,128]{3,2,1,0:T(8,128)S(1)}, f32[8,2,7,128]{3,2,1,0:T(8,128)}, u32[]{:S(2)}) copy-start(f32[8,2,7,128]{3,2,1,0:T(8,128)} %get-tuple-element.230) | copy-start | bytes 172036 | tf_op jit(solution)/shard_map/while/body/eval_jaxpr/cond
  27.1 2.7 %copy-start.1 = (f32[8,2,7,128,64]{3,4,2,1,0:T(8,128)S(1)}, f32[8,2,7,128,64]{3,4,2,1,0:T(8,128)}, u32[]{:S(2)}) copy-start(f32[8,2,7,128,64]{3,4,2,1,0:T(8,128)} %get-tuple-element.231) | copy-start | bytes 11010052 | tf_op jit(solution)/shard_map/while/body/eval_jaxpr/cond
  38.1 4.1 %collective-permute-start = (bf16[8,128,2,64]{1,3,2,0:T(8,128)(2,1)}, bf16[8,128,2,64]{1,3,2,0:T(8,128)(2,1)}, u32[]{:S(2)}, u32[]{:S(2)}) collective-permute-start(bf16[8,128,2,64]{1,3,2,0:T(8,128)(2,1)} %get-tuple-element.353), channel_id=1, source_target_pairs={{0,1},{1,2},{2,3},{3,4},{4,5},{5,6},{6,7},{7,0},{8,9},{9,10},{10,1... | collective-permute-start | bytes 786440 | tf_op jit(solution)/shard_map/while/body/eval_jaxpr/ppermute | solution.py:64
  38.1 6.1 %collective-permute-start.1 = (bf16[8,128,2,64]{1,3,2,0:T(8,128)(2,1)}, bf16[8,128,2,64]{1,3,2,0:T(8,128)(2,1)}, u32[]{:S(2)}, u32[]{:S(2)}) collective-permute-start(bf16[8,128,2,64]{1,3,2,0:T(8,128)(2,1)} %get-tuple-element.354), channel_id=1, source_target_pairs={{0,1},{1,2},{2,3},{3,4},{4,5},{5,6},{6,7},{7,0},{8,9},{9,10},{10,1... | collective-permute-start | bytes 786440 | tf_op jit(solution)/shard_map/while/body/eval_jaxpr/ppermute | solution.py:64
  46.4 2.0 %copy-start.3 = (f32[8,2,7,128]{3,2,1,0:T(8,128)S(1)}, f32[8,2,7,128]{3,2,1,0:T(8,128)}, u32[]{:S(2)}) copy-start(f32[8,2,7,128]{3,2,1,0:T(8,128)} %get-tuple-element.230) | copy-start | bytes 172036 | tf_op jit(solution)/shard_map/while/body/eval_jaxpr/cond
  46.4 2.7 %copy-start.1 = (f32[8,2,7,128,64]{3,4,2,1,0:T(8,128)S(1)}, f32[8,2,7,128,64]{3,4,2,1,0:T(8,128)}, u32[]{:S(2)}) copy-start(f32[8,2,7,128,64]{3,4,2,1,0:T(8,128)} %get-tuple-element.231) | copy-start | bytes 11010052 | tf_op jit(solution)/shard_map/while/body/eval_jaxpr/cond
  57.4 6.6 %collective-permute-start = (bf16[8,128,2,64]{1,3,2,0:T(8,128)(2,1)}, bf16[8,128,2,64]{1,3,2,0:T(8,128)(2,1)}, u32[]{:S(2)}, u32[]{:S(2)}) collective-permute-start(bf16[8,128,2,64]{1,3,2,0:T(8,128)(2,1)} %get-tuple-element.353), channel_id=1, source_target_pairs={{0,1},{1,2},{2,3},{3,4},{4,5},{5,6},{6,7},{7,0},{8,9},{9,10},{10,1... | collective-permute-start | bytes 786440 | tf_op jit(solution)/shard_map/while/body/eval_jaxpr/ppermute | solution.py:64
  57.4 7.0 %collective-permute-start.1 = (bf16[8,128,2,64]{1,3,2,0:T(8,128)(2,1)}, bf16[8,128,2,64]{1,3,2,0:T(8,128)(2,1)}, u32[]{:S(2)}, u32[]{:S(2)}) collective-permute-start(bf16[8,128,2,64]{1,3,2,0:T(8,128)(2,1)} %get-tuple-element.354), channel_id=1, source_target_pairs={{0,1},{1,2},{2,3},{3,4},{4,5},{5,6},{6,7},{7,0},{8,9},{9,10},{10,1... | collective-permute-start | bytes 786440 | tf_op jit(solution)/shard_map/while/body/eval_jaxpr/ppermute | solution.py:64
  66.5 2.0 %copy-start.3 = (f32[8,2,7,128]{3,2,1,0:T(8,128)S(1)}, f32[8,2,7,128]{3,2,1,0:T(8,128)}, u32[]{:S(2)}) copy-start(f32[8,2,7,128]{3,2,1,0:T(8,128)} %get-tuple-element.230) | copy-start | bytes 172036 | tf_op jit(solution)/shard_map/while/body/eval_jaxpr/cond
  66.5 2.7 %copy-start.1 = (f32[8,2,7,128,64]{3,4,2,1,0:T(8,128)S(1)}, f32[8,2,7,128,64]{3,4,2,1,0:T(8,128)}, u32[]{:S(2)}) copy-start(f32[8,2,7,128,64]{3,4,2,1,0:T(8,128)} %get-tuple-element.231) | copy-start | bytes 11010052 | tf_op jit(solution)/shard_map/while/body/eval_jaxpr/cond
  77.6 8.2 %collective-permute-start = (bf16[8,128,2,64]{1,3,2,0:T(8,128)(2,1)}, bf16[8,128,2,64]{1,3,2,0:T(8,128)(2,1)}, u32[]{:S(2)}, u32[]{:S(2)}) collective-permute-start(bf16[8,128,2,64]{1,3,2,0:T(8,128)(2,1)} %get-tuple-element.353), channel_id=1, source_target_pairs={{0,1},{1,2},{2,3},{3,4},{4,5},{5,6},{6,7},{7,0},{8,9},{9,10},{10,1... | collective-permute-start | bytes 786440 | tf_op jit(solution)/shard_map/while/body/eval_jaxpr/ppermute | solution.py:64
  77.6 8.6 %collective-permute-start.1 = (bf16[8,128,2,64]{1,3,2,0:T(8,128)(2,1)}, bf16[8,128,2,64]{1,3,2,0:T(8,128)(2,1)}, u32[]{:S(2)}, u32[]{:S(2)}) collective-permute-start(bf16[8,128,2,64]{1,3,2,0:T(8,128)(2,1)} %get-tuple-element.354), channel_id=1, source_target_pairs={{0,1},{1,2},{2,3},{3,4},{4,5},{5,6},{6,7},{7,0},{8,9},{9,10},{10,1... | collective-permute-start | bytes 786440 | tf_op jit(solution)/shard_map/while/body/eval_jaxpr/ppermute | solution.py:64
  88.3 2.0 %copy-start.3 = (f32[8,2,7,128]{3,2,1,0:T(8,128)S(1)}, f32[8,2,7,128]{3,2,1,0:T(8,128)}, u32[]{:S(2)}) copy-start(f32[8,2,7,128]{3,2,1,0:T(8,128)} %get-tuple-element.230) | copy-start | bytes 172036 | tf_op jit(solution)/shard_map/while/body/eval_jaxpr/cond
  88.4 2.7 %copy-start.1 = (f32[8,2,7,128,64]{3,4,2,1,0:T(8,128)S(1)}, f32[8,2,7,128,64]{3,4,2,1,0:T(8,128)}, u32[]{:S(2)}) copy-start(f32[8,2,7,128,64]{3,4,2,1,0:T(8,128)} %get-tuple-element.231) | copy-start | bytes 11010052 | tf_op jit(solution)/shard_map/while/body/eval_jaxpr/cond
  99.4 8.2 %collective-permute-start = (bf16[8,128,2,64]{1,3,2,0:T(8,128)(2,1)}, bf16[8,128,2,64]{1,3,2,0:T(8,128)(2,1)}, u32[]{:S(2)}, u32[]{:S(2)}) collective-permute-start(bf16[8,128,2,64]{1,3,2,0:T(8,128)(2,1)} %get-tuple-element.353), channel_id=1, source_target_pairs={{0,1},{1,2},{2,3},{3,4},{4,5},{5,6},{6,7},{7,0},{8,9},{9,10},{10,1... | collective-permute-start | bytes 786440 | tf_op jit(solution)/shard_map/while/body/eval_jaxpr/ppermute | solution.py:64
  99.4 8.6 %collective-permute-start.1 = (bf16[8,128,2,64]{1,3,2,0:T(8,128)(2,1)}, bf16[8,128,2,64]{1,3,2,0:T(8,128)(2,1)}, u32[]{:S(2)}, u32[]{:S(2)}) collective-permute-start(bf16[8,128,2,64]{1,3,2,0:T(8,128)(2,1)} %get-tuple-element.354), channel_id=1, source_target_pairs={{0,1},{1,2},{2,3},{3,4},{4,5},{5,6},{6,7},{7,0},{8,9},{9,10},{10,1... | collective-permute-start | bytes 786440 | tf_op jit(solution)/shard_map/while/body/eval_jaxpr/ppermute | solution.py:64
  110.2 2.0 %copy-start.3 = (f32[8,2,7,128]{3,2,1,0:T(8,128)S(1)}, f32[8,2,7,128]{3,2,1,0:T(8,128)}, u32[]{:S(2)}) copy-start(f32[8,2,7,128]{3,2,1,0:T(8,128)} %get-tuple-element.230) | copy-start | bytes 172036 | tf_op jit(solution)/shard_map/while/body/eval_jaxpr/cond
  110.2 2.7 %copy-start.1 = (f32[8,2,7,128,64]{3,4,2,1,0:T(8,128)S(1)}, f32[8,2,7,128,64]{3,4,2,1,0:T(8,128)}, u32[]{:S(2)}) copy-start(f32[8,2,7,128,64]{3,4,2,1,0:T(8,128)} %get-tuple-element.231) | copy-start | bytes 11010052 | tf_op jit(solution)/shard_map/while/body/eval_jaxpr/cond
  121.2 8.2 %collective-permute-start = (bf16[8,128,2,64]{1,3,2,0:T(8,128)(2,1)}, bf16[8,128,2,64]{1,3,2,0:T(8,128)(2,1)}, u32[]{:S(2)}, u32[]{:S(2)}) collective-permute-start(bf16[8,128,2,64]{1,3,2,0:T(8,128)(2,1)} %get-tuple-element.353), channel_id=1, source_target_pairs={{0,1},{1,2},{2,3},{3,4},{4,5},{5,6},{6,7},{7,0},{8,9},{9,10},{10,1... | collective-permute-start | bytes 786440 | tf_op jit(solution)/shard_map/while/body/eval_jaxpr/ppermute | solution.py:64
  121.2 8.6 %collective-permute-start.1 = (bf16[8,128,2,64]{1,3,2,0:T(8,128)(2,1)}, bf16[8,128,2,64]{1,3,2,0:T(8,128)(2,1)}, u32[]{:S(2)}, u32[]{:S(2)}) collective-permute-start(bf16[8,128,2,64]{1,3,2,0:T(8,128)(2,1)} %get-tuple-element.354), channel_id=1, source_target_pairs={{0,1},{1,2},{2,3},{3,4},{4,5},{5,6},{6,7},{7,0},{8,9},{9,10},{10,1... | collective-permute-start | bytes 786440 | tf_op jit(solution)/shard_map/while/body/eval_jaxpr/ppermute | solution.py:64
  132.0 2.0 %copy-start.3 = (f32[8,2,7,128]{3,2,1,0:T(8,128)S(1)}, f32[8,2,7,128]{3,2,1,0:T(8,128)}, u32[]{:S(2)}) copy-start(f32[8,2,7,128]{3,2,1,0:T(8,128)} %get-tuple-element.230) | copy-start | bytes 172036 | tf_op jit(solution)/shard_map/while/body/eval_jaxpr/cond
  132.0 2.7 %copy-start.1 = (f32[8,2,7,128,64]{3,4,2,1,0:T(8,128)S(1)}, f32[8,2,7,128,64]{3,4,2,1,0:T(8,128)}, u32[]{:S(2)}) copy-start(f32[8,2,7,128,64]{3,4,2,1,0:T(8,128)} %get-tuple-element.231) | copy-start | bytes 11010052 | tf_op jit(solution)/shard_map/while/body/eval_jaxpr/cond
  143.0 8.2 %collective-permute-start = (bf16[8,128,2,64]{1,3,2,0:T(8,128)(2,1)}, bf16[8,128,2,64]{1,3,2,0:T(8,128)(2,1)}, u32[]{:S(2)}, u32[]{:S(2)}) collective-permute-start(bf16[8,128,2,64]{1,3,2,0:T(8,128)(2,1)} %get-tuple-element.353), channel_id=1, source_target_pairs={{0,1},{1,2},{2,3},{3,4},{4,5},{5,6},{6,7},{7,0},{8,9},{9,10},{10,1... | collective-permute-start | bytes 786440 | tf_op jit(solution)/shard_map/while/body/eval_jaxpr/ppermute | solution.py:64
  143.0 8.6 %collective-permute-start.1 = (bf16[8,128,2,64]{1,3,2,0:T(8,128)(2,1)}, bf16[8,128,2,64]{1,3,2,0:T(8,128)(2,1)}, u32[]{:S(2)}, u32[]{:S(2)}) collective-permute-start(bf16[8,128,2,64]{1,3,2,0:T(8,128)(2,1)} %get-tuple-element.354), channel_id=1, source_target_pairs={{0,1},{1,2},{2,3},{3,4},{4,5},{5,6},{6,7},{7,0},{8,9},{9,10},{10,1... | collective-permute-start | bytes 786440 | tf_op jit(solution)/shard_map/while/body/eval_jaxpr/ppermute | solution.py:64
  153.8 2.0 %copy-start.3 = (f32[8,2,7,128]{3,2,1,0:T(8,128)S(1)}, f32[8,2,7,128]{3,2,1,0:T(8,128)}, u32[]{:S(2)}) copy-start(f32[8,2,7,128]{3,2,1,0:T(8,128)} %get-tuple-element.230) | copy-start | bytes 172036 | tf_op jit(solution)/shard_map/while/body/eval_jaxpr/cond
  153.8 2.7 %copy-start.1 = (f32[8,2,7,128,64]{3,4,2,1,0:T(8,128)S(1)}, f32[8,2,7,128,64]{3,4,2,1,0:T(8,128)}, u32[]{:S(2)}) copy-start(f32[8,2,7,128,64]{3,4,2,1,0:T(8,128)} %get-tuple-element.231) | copy-start | bytes 11010052 | tf_op jit(solution)/shard_map/while/body/eval_jaxpr/cond
  (16 other events, 19.9 us)
where the time goes:
time: 172 us; the launch traced here: 171 us
  matrix products  54 us (31%)
  waiting for transfers between devices  51.5 us (30%)
  local copies, waits for them, and re-layouts  40.6 us (24%)
  other arithmetic  22.2 us (13%)
  starting transfers between devices  2.06 us (1%)
    ppermute x14, waiting for transfers between devices, step_fn(): k_blk, v_blk = lax.ppermute((k_blk, v_blk), 'cp', shift_pairs)  51.5 us
    dot_general x8, matrix products, attend_block(): jnp.einsum('bkgqs,bskd->bkgqd', prob_blk, v_blk, preferred_element_type=j...  25.9 us
    while x14, local copies, waits for them, and re-layouts  23.4 us
    cond x63, local copies, waits for them, and re-layouts  16.9 us
    reduce_sum x8, other arithmetic, attend_block(): new_sum = run_sum * rescale + jnp.sum(prob_blk, axis=-1)  16.2 us
    dot_general x8, matrix products, attend_block(): jnp.einsum('bqkgd,bskd->bkgqs', q_grp, k_blk, preferred_element_type=jnp....  16 us
    dot_general x1, matrix products, local_block(): jnp.einsum('bkgqd,kgde->bqe', attn_out, w_out.reshape(n_kv, n_groups, hea...  6.21 us
    dot_general x1, matrix products, local_block(): jnp.einsum('bsd,de->bse', normed, w_query, preferred_element_type=jnp.flo...  4.25 us
  transfers between devices with their start and end apart: 14, of which 14 were waited for; matrix products, arithmetic and copies ran while one was open for 0% of the time, Pallas kernels for 0%

commit v1 on v0

v1 whole, which is shorter than its diff:
```python
import functools

import jax
import jax.numpy as jnp
import numpy as np
from jax import lax
from jax.experimental import pallas as pl
from jax.experimental.pallas import tpu as pltpu
from jax.sharding import PartitionSpec as P

F32 = jnp.float32
BF16 = jnp.bfloat16
MESH = pl.DeviceIdType.MESH
S_PART, S_RIGHT, S_LEFT, S_RELAY, S_FWD = 0, 1, 2, 3, 4
AHEAD = 3


def tdot(lhs, rhs, dims):
    return lax.dot_general(lhs, rhs, (dims, ((), ())), preferred_element_type=F32)


def rope(proj, cos, sin):
    half = cos.shape[0]
    first, second = proj[:half], proj[half:]
    return jnp.concatenate([first * cos - second * sin, second * cos + first * sin], axis=0).astype(BF16)


def block_kernel(n_cp, x_hbm, pos_ref, gain_ref, freq_ref, wq_hbm, wk_hbm, wv_hbm, wo_hbm, y_hbm,
                 x_s, wq_s, wk_s, wv_s, wo_s, cos_s, sin_s, q_s, kv_s, score_s, bias_s, ot_s, y_s,
                 x_sem, w_sem, y_sem, send_sem, recv_sem):
    batch, tok, dim = x_hbm.shape
    head = 2 * freq_ref.shape[0]
    n_heads = wq_hbm.shape[1] // head
    n_kv = wk_hbm.shape[1] // head
    group = n_heads // n_kv
    n_pairs = n_heads // 2
    n_chips = n_cp // 2
    scale = float(head ** -0.5 * np.log2(np.e))

    me = lax.axis_index('cp')
    chip = me // 2
    core = me % 2
    partner = chip * 2 + 1 - core

    def x_copy(b):
        return pltpu.make_async_copy(x_hbm.at[b], x_s.at[b], x_sem.at[b])

    w_copies = [pltpu.make_async_copy(src, dst, w_sem.at[i]) for i, (src, dst) in enumerate(
        ((wk_hbm, wk_s), (wv_hbm, wv_s), (wq_hbm, wq_s), (wo_hbm, wo_s)))]
    x_copy(0).start()
    x_copy(1).start()
    w_copies[0].start()
    w_copies[1].start()
    w_copies[2].start()
    for b in range(2, batch):
        x_copy(b).start()
    w_copies[3].start()

    barrier = pltpu.get_barrier_semaphore()
    for d in range(1, n_cp):
        pl.semaphore_signal(barrier, inc=1, device_id={'cp': lax.rem(me + d, n_cp)}, device_id_type=MESH)

    for b in range(batch):
        angle = pos_ref[pl.ds(b, 1), :].astype(F32) * freq_ref[...]
        cos_s[:, b * tok:(b + 1) * tok] = jnp.cos(angle)
        sin_s[:, b * tok:(b + 1) * tok] = jnp.sin(angle)
    q_s[...] = jnp.zeros_like(q_s)
    key_i = lax.broadcasted_iota(jnp.int32, bias_s.shape, 0)
    tok_i = lax.broadcasted_iota(jnp.int32, bias_s.shape, 1)
    bias_s[...] = jnp.where(key_i <= tok_i + core * tok, 0.0, -jnp.inf).astype(F32)

    pl.semaphore_wait(barrier, n_cp - 1)

    def send(b, src, dst, kind):
        return pltpu.make_async_remote_copy(
            src_ref=kv_s.at[b, src], dst_ref=kv_s.at[b, src],
            send_sem=send_sem.at[kind, b], recv_sem=recv_sem.at[b, src],
            device_id={'cp': dst}, device_id_type=MESH)

    def wait_recv(b, src):
        send(b, src, partner, S_PART).wait_recv()

    def via_left(b):
        return (b + core) % 2 == 1

    def each_own(b, do):
        do(send(b, me, partner, S_PART))

        @pl.when(chip == 0)
        def _():
            do(send(b, me, 6 + core, S_LEFT))
            do(send(b, me, 2 + core, S_RIGHT))

        @pl.when(chip == 1)
        def _():
            @pl.when(via_left(b))
            def _():
                do(send(b, me, core, S_LEFT))
            do(send(b, me, 4 + core, S_RIGHT))

        @pl.when(chip == 2)
        def _():
            do(send(b, me, 6 + core, S_RIGHT))

    def relays(b, first, then):
        def forward(c):
            then(send(b, 2 * c + core, partner, S_FWD + c))

        @pl.when(chip == 0)
        def _():
            @pl.when(via_left(b))
            def _():
                first(2 + core)
                then(send(b, 2 + core, 6 + core, S_RELAY))

        @pl.when(chip == 1)
        def _():
            first(core)
            forward(0)

        @pl.when(chip == 2)
        def _():
            first(2 + core)

            @pl.when(jnp.logical_not(via_left(b)))
            def _():
                then(send(b, 2 + core, 6 + core, S_RELAY))
            forward(1)
            first(core)
            forward(0)

        @pl.when(chip == 3)
        def _():
            first(core)
            then(send(b, core, 4 + core, S_RELAY))
            forward(0)
            first(4 + core)
            forward(2)
            first(2 + core)
            forward(1)

    w_copies[0].wait()
    w_copies[1].wait()

    def project(p, first_pair):
        for i in range(2):
            x_copy(2 * p + i).wait()
        x_pair = x_s[pl.ds(2 * p, 2)].reshape(2 * tok, dim).astype(F32)
        inv_rms = lax.rsqrt(jnp.mean(x_pair * x_pair, axis=-1, keepdims=True) + 1e-5)
        normed = (x_pair * inv_rms * gain_ref[...].astype(F32)).astype(BF16)
        lanes = pl.ds(pl.multiple_of(p * 2 * tok, 2 * tok), 2 * tok)
        cos, sin = cos_s[:, lanes], sin_s[:, lanes]
        k_t = tdot(wk_s[...], normed, ((0,), (1,)))
        v_t = tdot(wv_s[...], normed, ((0,), (1,))).astype(BF16)
        k_rot = jnp.concatenate([rope(k_t[g * head:(g + 1) * head], cos, sin) for g in range(n_kv)], axis=0)
        for i in range(2):
            kv_s[2 * p + i, me, 0] = k_rot[:, i * tok:(i + 1) * tok].T
            kv_s[2 * p + i, me, 1] = v_t[:, i * tok:(i + 1) * tok]
        for i in range(2):
            @pl.when(2 * p + i < AHEAD)
            def _():
                each_own(2 * p + i, lambda copy: copy.start())
        if first_pair:
            w_copies[2].wait()
        q_t = tdot(wq_s[...], normed, ((0,), (1,)))
        for n in range(n_heads):
            q_rot = rope(q_t[n * head:(n + 1) * head], cos, sin)
            row = (n // group) * head
            col = (n % 2) * tok
            for i in range(2):
                q_s[2 * p + i, n // 2, row:row + head, col:col + tok] = q_rot[:, i * tok:(i + 1) * tok]

    project(0, True)

    @pl.loop(1, batch // 2)
    def _(p):
        project(p, False)

    w_copies[3].wait()

    def attend(b, chunks):
        keys = 2 * tok * chunks
        for t in range(n_pairs):
            q_pair = q_s[b, t]
            slot = t % 2
            for c in range(chunks):
                k_blk = jnp.concatenate([kv_s[b, 2 * c, 0], kv_s[b, 2 * c + 1, 0]], axis=0)
                s_blk = tdot(k_blk, q_pair, ((1,), (0,)))
                if c == chunks - 1:
                    bias = bias_s[...]
                    s_blk = s_blk + jnp.concatenate([bias, bias], axis=1)
                score_s[slot, 2 * tok * c:2 * tok * (c + 1)] = s_blk
                part = jnp.max(s_blk, axis=0, keepdims=True)
                top = part if c == 0 else jnp.maximum(top, part)
            prob = jnp.exp2((score_s[slot, :keys] - top) * scale)
            total = jnp.sum(prob, axis=0, keepdims=True)
            lo, hi = (2 * t) // group, (2 * t + 1) // group
            v_rows = slice(lo * head, (hi + 1) * head)
            v_blk = jnp.concatenate([kv_s[b, s, 1][v_rows] for s in range(2 * chunks)], axis=1)
            out = tdot(v_blk, prob.astype(BF16), ((1,), (0,)))
            inv = 1.0 / total
            for i in range(2):
                n = 2 * t + i
                row = (n // group - lo) * head
                cols = slice(i * tok, (i + 1) * tok)
                ot_s[n * head:(n + 1) * head] = (out[row:row + head, cols] * inv[:, cols]).astype(BF16)

    def y_copy(b):
        return pltpu.make_async_copy(y_s.at[b], y_hbm.at[b], y_sem.at[b])

    @pl.loop(0, batch)
    def _(b):
        relays(b, lambda src: wait_recv(b, src), lambda copy: copy.start())

        @pl.when(b + AHEAD < batch)
        def _():
            each_own(b + AHEAD, lambda copy: copy.start())
        wait_recv(b, partner)
        for j in range(n_chips):
            @pl.when(chip == j)
            def _():
                for c in range(j):
                    wait_recv(b, 2 * c + 1 - core)
                attend(b, j + 1)
        proj = tdot(ot_s[...], wo_s[...], ((0,), (0,)))
        y_s[b] = (x_s[b].astype(F32) + proj).astype(BF16)
        y_copy(b).start()

    @pl.loop(0, batch)
    def _(b):
        y_copy(b).wait()
        each_own(b, lambda copy: copy.wait_send())
        relays(b, lambda src: None, lambda copy: copy.wait_send())


def solution(mesh):
    n_cp = mesh.shape['cp']

    def local_block(hidden, positions, norm_gain, w_query, w_key, w_value, w_out):
        batch, tok, dim = hidden.shape
        n_heads, head, _ = w_out.shape
        kv_dim = w_key.shape[1]
        freq = np.float32(10000.0) ** (np.float32(-2.0) * np.arange(head // 2, dtype=np.float32) / np.float32(head))
        freq = jnp.asarray(np.broadcast_to(freq.astype(np.float32)[:, None], (head // 2, tok)))
        hbm = pl.BlockSpec(memory_space=pl.ANY)
        vmem = pl.BlockSpec(memory_space=pltpu.VMEM)
        flops = 2 * batch * tok * dim * (2 * dim + 2 * kv_dim) + 4 * batch * tok * n_cp * tok * n_heads * head
        return pl.pallas_call(
            functools.partial(block_kernel, n_cp),
            name='attention_block',
            out_shape=jax.ShapeDtypeStruct(hidden.shape, hidden.dtype),
            in_specs=[hbm, vmem, vmem, vmem, hbm, hbm, hbm, hbm],
            out_specs=hbm,
            scratch_shapes=[
                pltpu.VMEM(hidden.shape, BF16),
                pltpu.VMEM(w_query.shape, BF16),
                pltpu.VMEM(w_key.shape, BF16),
                pltpu.VMEM(w_value.shape, BF16),
                pltpu.VMEM((n_heads * head, dim), BF16),
                pltpu.VMEM((head // 2, batch * tok), F32),
                pltpu.VMEM((head // 2, batch * tok), F32),
                pltpu.VMEM((batch, n_heads // 2, kv_dim, 2 * tok), BF16),
                pltpu.VMEM((batch, n_cp, 2, tok, kv_dim), BF16),
                pltpu.VMEM((2, n_cp * tok, 2 * tok), F32),
                pltpu.VMEM((2 * tok, tok), F32),
                pltpu.VMEM((n_heads * head, tok), BF16),
                pltpu.VMEM(hidden.shape, BF16),
                pltpu.SemaphoreType.DMA((batch,)),
                pltpu.SemaphoreType.DMA((4,)),
                pltpu.SemaphoreType.DMA((batch,)),
                pltpu.SemaphoreType.DMA((S_FWD + n_cp // 2 - 1, batch)),
                pltpu.SemaphoreType.DMA((batch, n_cp)),
            ],
            compiler_params=pltpu.CompilerParams(
                collective_id=0, has_side_effects=True, vmem_limit_bytes=56 * 1024 * 1024),
            cost_estimate=pl.CostEstimate(flops=flops, bytes_accessed=8_000_000, transcendentals=0),
        )(hidden, positions, norm_gain.reshape(1, dim), freq, w_query, w_key, w_value, w_out.reshape(n_heads * head, dim))

    act_spec = P('dp', 'cp', None)
    return jax.shard_map(local_block, mesh=mesh, in_specs=(act_spec, P('dp', 'cp'), P(), P(), P(), P(), P()), out_specs=act_spec, check_vma=False)
```

time: 172 us -> 73.9 us (0.43)
  the two profiles are of different devices: /device:TPU:119 before, /device:TPU:117 now
where the time goes in v1:
time: 73.9 us; the launch traced here: 73.7 us
  Pallas kernels  68.3 us (92%)
  local copies, waits for them, and re-layouts  5.48 us (7%)
    pallas_call x1, Pallas kernels, local_block(): pl.pallas_call(functools.partial(block_kernel, n_cp), name='attention_blo...  68.3 us
    unnamed x1, local copies, waits for them, and re-layouts  2.88 us

profile of v1, /device:TPU:117, one launch (start us, length us, event | category | flops | bytes accessed | tf_op | source)
XLA Modules:
  0.0 73.7 jit_solution(12789250079538339491)
XLA Ops:
  0.0 1.3 %reshape.6.gain_ref = bf16[1,896]{1,0:T(2,128)(2,1)} reshape(bf16[896]{0:T(1024)(128)(2,1)} %param.10) | data formatting | bytes 3584 | tf_op jit(solution)/shard_map/reshape | solution.py:277
  1.3 1.3 %jit_solution_.3.freq_ref = f32[32,128]{1,0:T(8,128)} broadcast(f32[32]{0:T(128)} %constant.2.clone), dimensions={0} | broadcast | bytes 16512 | tf_op jit(solution)
  2.6 68.3 %attention_block.1 = bf16[8,128,896]{2,1,0:T(8,128)(2,1)} custom-call(bf16[8,128,896]{2,1,0:T(8,128)(2,1)} %x_hbm.1, s32[8,128]{1,0:T(8,128)} %pos_ref.1, bf16[1,896]{1,0:T(2,128)(2,1)} %reshape.6.gain_ref, f32[32,128]{1,0:T(8,128)} %jit_solution_.3.freq_ref, bf16[896,896]{1,0:T(8,128)(2,1)} %wq_hbm.1, bf16[896,128]{1,0:T(8,128)(2,1)} %wk_hbm.1, ...), custom_call_target="tpu_custom_call" | custom-call | flops 7516192768 | bytes 8000000 | tf_op jit(solution)/shard_map/attention_block/pallas_call | solution.py:248
  70.9 2.9 %copy.10 = bf16[8,128,896]{2,1,0:T(8,128)(2,1)} copy(bf16[8,128,896]{2,1,0:T(8,128)(2,1)} %attention_block.1) | data formatting | bytes 3670016

commit v2 on v1

v2 whole, which is shorter than its diff:
```python
import functools

import jax
import jax.numpy as jnp
import numpy as np
from jax import lax
from jax.experimental import pallas as pl
from jax.experimental.pallas import tpu as pltpu
from jax.sharding import PartitionSpec as P

F32 = jnp.float32
BF16 = jnp.bfloat16
MESH = pl.DeviceIdType.MESH
S_PART, S_RIGHT, S_LEFT, S_FAR, S_RELAY, S_FWD = 0, 1, 2, 3, 4, 5
AHEAD = 3
PACED = (2, 2, 4, 2)
SPLIT = 4


def tdot(lhs, rhs, dims):
    return lax.dot_general(lhs, rhs, (dims, ((), ())), preferred_element_type=F32)


def rope(proj, cos, sin):
    half = cos.shape[0]
    first, second = proj[:half], proj[half:]
    return jnp.concatenate([first * cos - second * sin, second * cos + first * sin], axis=0).astype(BF16)


def block_kernel(n_cp, head, x_hbm, pos_hbm, gain_hbm, wq_hbm, wk_hbm, wv_hbm, wo_hbm, y_ref,
                 pos_ref, gain_ref, freq_s, x_s, wq_s, wk_s, wv_s, wo_s, q_s, kv_s, score_s, bias_s, o_s,
                 x_sem, w_sem, send_sem, recv_sem):
    batch, tok, dim = x_hbm.shape
    kv_dim = wk_hbm.shape[1]
    n_kv = kv_dim // head
    n_heads = wq_hbm.shape[1] // head
    group = n_heads // n_kv
    n_pairs = n_heads // 2
    n_chips = n_cp // 2
    scale = float(head ** -0.5 * np.log2(np.e))

    me = lax.axis_index('cp')
    chip = me // 2
    core = me % 2
    partner = chip * 2 + 1 - core

    def x_copy(b):
        return pltpu.make_async_copy(x_hbm.at[b], x_s.at[b], x_sem.at[b])

    w_copies = [pltpu.make_async_copy(src, dst, w_sem.at[i]) for i, (src, dst) in enumerate(
        ((wk_hbm, wk_s), (wv_hbm, wv_s), (wq_hbm, wq_s), (wo_hbm, wo_s), (pos_hbm, pos_ref), (gain_hbm, gain_ref)))]
    w_copies[4].start()
    x_copy(0).start()
    x_copy(1).start()
    w_copies[5].start()
    w_copies[0].start()
    w_copies[1].start()
    w_copies[2].start()
    for b in range(2, batch):
        x_copy(b).start()
    w_copies[3].start()

    barrier = pltpu.get_barrier_semaphore()
    for d in range(1, n_cp):
        pl.semaphore_signal(barrier, inc=1, device_id={'cp': lax.rem(me + d, n_cp)}, device_id_type=MESH)

    key_i = lax.broadcasted_iota(jnp.int32, bias_s.shape, 0)
    tok_i = lax.broadcasted_iota(jnp.int32, bias_s.shape, 1)
    bias_s[...] = jnp.where(key_i <= tok_i + core * tok, 0.0, -jnp.inf).astype(F32)

    def send(b, src, dst, kind):
        return pltpu.make_async_remote_copy(
            src_ref=kv_s.at[b, src], dst_ref=kv_s.at[b, src],
            send_sem=send_sem.at[kind, b], recv_sem=recv_sem.at[b, src],
            device_id={'cp': dst}, device_id_type=MESH)

    def wait_recv(b, src):
        send(b, src, partner, S_PART).wait_recv()

    def on_chip(do):
        for j in range(n_chips):
            @pl.when(chip == j)
            def _():
                do(j)

    def direct_0_to_2(b):
        return (b < 2) | (b >= 6)

    def direct_1_to_3(b):
        return b < 4

    def own(j, b, do):
        if j == 0:
            do(send(b, me, 6 + core, S_LEFT))
            do(send(b, me, 2 + core, S_RIGHT))

            @pl.when(direct_0_to_2(b))
            def _():
                do(send(b, me, 4 + core, S_FAR))
        if j == 1:
            @pl.when(direct_1_to_3(b))
            def _():
                do(send(b, me, 6 + core, S_FAR))
            do(send(b, me, 4 + core, S_RIGHT))
        if j == 2:
            do(send(b, me, 6 + core, S_RIGHT))

    def stages(j, first, then):
        def forward(b, c):
            then(send(b, 2 * c + core, partner, S_FWD + c))

        def near(b):
            first(b, 2 * (j - 1) + core)
            forward(b, j - 1)

        def chip_2_right(b):
            first(b, 2 + core)

            @pl.when(jnp.logical_not(direct_1_to_3(b)))
            def _():
                then(send(b, 2 + core, 6 + core, S_RELAY))
            forward(b, 1)

        def chip_2_left(b):
            first(b, core)
            forward(b, 0)

        def chip_3(b):
            first(b, core)

            @pl.when(jnp.logical_not(direct_0_to_2(b)))
            def _():
                then(send(b, core, 4 + core, S_RELAY))
            forward(b, 0)
            near(b)
            first(b, 2 + core)
            forward(b, 1)

        return ((), ((1, near),), ((AHEAD, chip_2_right), (1, chip_2_left)), ((1, chip_3),))[j]

    w_copies[4].wait()
    w_copies[5].wait()
    row_i = lax.broadcasted_iota(jnp.int32, (head // 2, 2 * tok), 0)
    freq = jnp.ones((head // 2, 2 * tok), F32)
    for j in range(1, head // 2):
        freq = jnp.where(row_i == j, F32(10000.0 ** (-2.0 * j / head)), freq)
    freq_s[...] = freq
    w_copies[0].wait()
    w_copies[1].wait()

    def project(p, first_pair):
        for i in range(2):
            x_copy(2 * p + i).wait()
        x_pair = x_s[pl.ds(2 * p, 2)].reshape(2 * tok, dim).astype(F32)
        inv_rms = lax.rsqrt(jnp.mean(x_pair * x_pair, axis=-1, keepdims=True) + 1e-5)
        normed = (x_pair * inv_rms * gain_ref[...].astype(F32).reshape(1, dim)).astype(BF16)
        pos = jnp.concatenate([pos_ref[pl.ds(2 * p + i, 1), :] for i in range(2)], axis=1)
        angle = pos.astype(F32) * freq_s[...]
        cos, sin = jnp.cos(angle), jnp.sin(angle)
        k_t = tdot(wk_s[...], normed, ((0,), (1,)))
        v_t = tdot(wv_s[...], normed, ((0,), (1,))).astype(BF16)
        k_rot = jnp.concatenate([rope(k_t[g * head:(g + 1) * head], cos, sin) for g in range(n_kv)], axis=0)
        for i in range(2):
            kv_s[2 * p + i, me, 0] = k_rot[:, i * tok:(i + 1) * tok].T
            kv_s[2 * p + i, me, 1] = v_t[:, i * tok:(i + 1) * tok]
        if first_pair:
            pl.semaphore_wait(barrier, n_cp - 1)

        def start_own(j):
            for i in range(2):
                @pl.when(2 * p + i < PACED[j])
                def _():
                    own(j, 2 * p + i, lambda copy: copy.start())
                send(2 * p + i, me, partner, S_PART).start()
        on_chip(start_own)
        if first_pair:
            w_copies[2].wait()
        q_t = tdot(wq_s[...], normed, ((0,), (1,)))
        zeros = jnp.zeros((head, tok), BF16)
        for n in range(n_heads):
            q_rot = rope(q_t[n * head:(n + 1) * head], cos, sin).astype(F32) * scale
            high = q_rot.astype(BF16)
            low = (q_rot - high.astype(F32)).astype(BF16)
            col = (n % 2) * tok
            for i in range(2):
                for part, q_part in enumerate((high, low)):
                    for g in range(n_kv):
                        q_s[2 * p + i, n // 2, part, g * head:(g + 1) * head, col:col + tok] = (
                            q_part[:, i * tok:(i + 1) * tok] if g == n // group else zeros)

    project(0, True)

    @pl.loop(1, batch // 2)
    def _(p):
        project(p, False)

    w_copies[3].wait()

    def scores(b, t, c, chunks):
        k_blk = jnp.concatenate([kv_s[b, 2 * c, 0], kv_s[b, 2 * c + 1, 0]], axis=0)
        s_blk = tdot(jnp.concatenate([k_blk, k_blk], axis=1), q_s[b, t].reshape(2 * kv_dim, 2 * tok), ((1,), (0,)))
        if c == chunks - 1:
            bias = bias_s[...]
            s_blk = s_blk + jnp.concatenate([bias, bias], axis=1)
        score_s[t % 2, 2 * tok * c:2 * tok * (c + 1)] = s_blk
        return jnp.max(s_blk, axis=0, keepdims=True)

    def attend(b, chunks, between):
        top = functools.reduce(jnp.maximum, [scores(b, 0, c, chunks) for c in range(chunks)])
        for t in range(n_pairs):
            if t == SPLIT:
                between()
            probs, total, next_top = [], None, None
            for c in range(chunks):
                if t + 1 < n_pairs:
                    part = scores(b, t + 1, c, chunks)
                    next_top = part if c == 0 else jnp.maximum(next_top, part)
                prob = jnp.exp2(score_s[t % 2, 2 * tok * c:2 * tok * (c + 1)] - top)
                part = jnp.sum(prob, axis=0, keepdims=True)
                total = part if c == 0 else total + part
                probs.append(prob)
            lo, hi = (2 * t) // group, (2 * t + 1) // group
            v_rows = slice(lo * head, (hi + 1) * head)
            v_blk = jnp.concatenate([kv_s[b, s, 1][v_rows] for s in range(2 * chunks)], axis=1)
            out = tdot(v_blk, jnp.concatenate(probs, axis=0), ((1,), (0,)))
            inv = 1.0 / total
            halves = []
            for i in range(2):
                row = ((2 * t + i) // group - lo) * head
                cols = slice(i * tok, (i + 1) * tok)
                halves.append(out[row:row + head, cols] * inv[:, cols])
            o_s[:, 2 * t * head:2 * (t + 1) * head] = jnp.concatenate(halves, axis=0).T.astype(BF16)
            top = next_top

    def pass_on(j):
        return stages(j, wait_recv, lambda copy: copy.start())

    def prologue(j):
        for ahead, stage in pass_on(j):
            for b in range(ahead):
                stage(jnp.int32(b))

    on_chip(prologue)

    @pl.loop(0, batch)
    def _(b):
        def one_chip(j):
            @pl.when(b + PACED[j] < batch)
            def _():
                own(j, b + PACED[j], lambda copy: copy.start())
            wait_recv(b, partner)
            for c in range(j):
                wait_recv(b, 2 * c + 1 - core)

            def between():
                for ahead, stage in pass_on(j):
                    @pl.when(b + ahead < batch)
                    def _():
                        stage(b + ahead)
            attend(b, j + 1, between)

        on_chip(one_chip)
        proj = tdot(o_s[...], wo_s[...], ((1,), (0,)))
        y_ref[b] = (x_s[b].astype(F32) + proj).astype(BF16)

    @pl.loop(0, batch)
    def _(b):
        def one_chip(j):
            send(b, me, partner, S_PART).wait_send()
            own(j, b, lambda copy: copy.wait_send())
            for _, stage in stages(j, lambda b, src: None, lambda copy: copy.wait_send()):
                stage(b)
        on_chip(one_chip)


def solution(mesh):
    n_cp = mesh.shape['cp']

    def local_block(hidden, positions, norm_gain, w_query, w_key, w_value, w_out):
        batch, tok, dim = hidden.shape
        n_heads, head, _ = w_out.shape
        kv_dim = w_key.shape[1]
        hbm = pl.BlockSpec(memory_space=pltpu.HBM)
        vmem = pl.BlockSpec(memory_space=pltpu.VMEM)
        flops = 2 * batch * tok * dim * (2 * dim + 2 * kv_dim) + 4 * batch * tok * n_cp * tok * n_heads * head
        return pl.pallas_call(
            functools.partial(block_kernel, n_cp, head),
            name='attention_block',
            out_shape=pltpu.VMEM(hidden.shape, hidden.dtype),
            in_specs=[hbm] * 7,
            out_specs=vmem,
            scratch_shapes=[
                pltpu.VMEM(positions.shape, jnp.int32),
                pltpu.VMEM(norm_gain.shape, BF16),
                pltpu.VMEM((head // 2, 2 * tok), F32),
                pltpu.VMEM(hidden.shape, BF16),
                pltpu.VMEM(w_query.shape, BF16),
                pltpu.VMEM(w_key.shape, BF16),
                pltpu.VMEM(w_value.shape, BF16),
                pltpu.VMEM((n_heads * head, dim), BF16),
                pltpu.VMEM((batch, n_heads // 2, 2, kv_dim, 2 * tok), BF16),
                pltpu.VMEM((batch, n_cp, 2, tok, kv_dim), BF16),
                pltpu.VMEM((2, n_cp * tok, 2 * tok), F32),
                pltpu.VMEM((2 * tok, tok), F32),
                pltpu.VMEM((tok, n_heads * head), BF16),
                pltpu.SemaphoreType.DMA((batch,)),
                pltpu.SemaphoreType.DMA((6,)),
                pltpu.SemaphoreType.DMA((S_FWD + n_cp // 2 - 1, batch)),
                pltpu.SemaphoreType.DMA((batch, n_cp)),
            ],
            compiler_params=pltpu.CompilerParams(
                collective_id=0, has_side_effects=True, vmem_limit_bytes=32 * 1024 * 1024),
            cost_estimate=pl.CostEstimate(flops=flops, bytes_accessed=8_000_000, transcendentals=0),
        )(*[pltpu.with_memory_space_constraint(arg, pltpu.HBM) for arg in (
            hidden, positions, norm_gain, w_query, w_key, w_value, w_out.reshape(n_heads * head, dim))])

    act_spec = P('dp', 'cp', None)
    return jax.shard_map(local_block, mesh=mesh, in_specs=(act_spec, P('dp', 'cp'), P(), P(), P(), P(), P()), out_specs=act_spec, check_vma=False)
```

time: 73.9 us -> 40.1 us (0.54)
  Pallas kernels: 68.3 us -> 38.8 us
  local copies, waits for them, and re-layouts: 5.48 us -> 1.23 us
    pallas_call x1, Pallas kernels: 68.3 us -> 38.8 us  [local_block(): pl.pallas_call(functools.partial(block_kernel, n_cp, head), name='attenti...]
    unnamed x1, local copies, waits for them, and re-layouts: 2.88 us -> 1.23 us
    another operation x1 -> x0, local copies, waits for them, and re-layouts: 1.33 us -> none
    reshape x1 -> x0, local copies, waits for them, and re-layouts: 1.28 us -> none  [local_block(): norm_gain.reshape(1, dim)]
where the time goes in v2:
time: 40.1 us; the launch traced here: 40 us
  Pallas kernels  38.8 us (97%)
  local copies, waits for them, and re-layouts  1.23 us (3%)
    pallas_call x1, Pallas kernels, local_block(): pl.pallas_call(functools.partial(block_kernel, n_cp, head), name='attenti...  38.8 us
    unnamed x1, local copies, waits for them, and re-layouts  1.23 us

profile of v2, /device:TPU:117, one launch (start us, length us, event | category | flops | bytes accessed | tf_op | source)
XLA Modules:
  0.0 40.0 jit_solution(15157595794773915177)
XLA Ops:
  0.0 38.8 %attention_block.1 = bf16[8,128,896]{2,1,0:T(8,128)(2,1)S(1)} custom-call(bf16[8,128,896]{2,1,0:T(8,128)(2,1)} %x_hbm.1, s32[8,128]{1,0:T(8,128)} %pos_hbm.1, bf16[896]{0:T(1024)(128)(2,1)} %gain_hbm.1, bf16[896,896]{1,0:T(8,128)(2,1)} %wq_hbm.1, bf16[896,128]{1,0:T(8,128)(2,1)} %wk_hbm.1, bf16[896,128]{1,0:T(8,128)(2,1)} %wv_hbm.1, bf16[896,896]{1,0:T(8,128)(2,1)} %bitcast.1), custom_call_target="tpu_custom_call" | custom-call | flops 7516192768 | bytes 8000000 | tf_op jit(solution)/shard_map/attention_block/pallas_call | solution.py:286
  38.8 1.2 %copy.9 = bf16[8,128,896]{2,1,0:T(8,128)(2,1)} copy(bf16[8,128,896]{2,1,0:T(8,128)(2,1)S(1)} %attention_block.1) | data formatting | bytes 3670016

commit v3 on v2

--- a/solution.py
+++ b/solution.py
@@ -12,9 +12,18 @@
 BF16 = jnp.bfloat16
 MESH = pl.DeviceIdType.MESH
 S_PART, S_RIGHT, S_LEFT, S_FAR, S_RELAY, S_FWD = 0, 1, 2, 3, 4, 5
-AHEAD = 3
-PACED = (2, 2, 4, 2)
-SPLIT = 4
+AHEAD_2, AHEAD_3 = 3, 2
+PACED = (3, 2, 3, 2)
+FAR_0_TO_2 = (3, 4, 6, 7)
+FAR_1_TO_3 = (5, 6, 7)
+HALF_FAR_1_TO_3 = (0, 3, 4)
+
+
+def one_of(b, numbers):
+    return functools.reduce(jnp.logical_or, [b == number for number in numbers], b < 0)
+
+
+SPLIT = 2
 
 
 def tdot(lhs, rhs, dims):
@@ -28,7 +37,7 @@
 
 
 def block_kernel(n_cp, head, x_hbm, pos_hbm, gain_hbm, wq_hbm, wk_hbm, wv_hbm, wo_hbm, y_ref,
-                 pos_ref, gain_ref, freq_s, x_s, wq_s, wk_s, wv_s, wo_s, q_s, kv_s, score_s, bias_s, o_s,
+                 pos_ref, gain_ref, freq_s, cos_s, sin_s, normed_s, x_s, wq_s, wk_s, wv_s, wo_s, q_s, kv_s, score_s, bias_s, o_s,
                  x_sem, w_sem, send_sem, recv_sem):
     batch, tok, dim = x_hbm.shape
     kv_dim = wk_hbm.shape[1]
@@ -84,10 +93,10 @@
                 do(j)
 
     def direct_0_to_2(b):
-        return (b < 2) | (b >= 6)
+        return one_of(b, FAR_0_TO_2)
 
     def direct_1_to_3(b):
-        return b < 4
+        return one_of(b, FAR_1_TO_3) | ((core == 0) & one_of(b, HALF_FAR_1_TO_3))
 
     def own(j, b, do):
         if j == 0:
@@ -125,18 +134,20 @@
             first(b, core)
             forward(b, 0)
 
-        def chip_3(b):
+        def chip_3_left(b):
             first(b, core)
 
             @pl.when(jnp.logical_not(direct_0_to_2(b)))
             def _():
                 then(send(b, core, 4 + core, S_RELAY))
             forward(b, 0)
+
+        def chip_3_right(b):
             near(b)
             first(b, 2 + core)
             forward(b, 1)
 
-        return ((), ((1, near),), ((AHEAD, chip_2_right), (1, chip_2_left)), ((1, chip_3),))[j]
+        return ((), ((1, near),), ((AHEAD_2, chip_2_right), (1, chip_2_left)), ((AHEAD_3, chip_3_left), (1, chip_3_right)))[j]
 
     w_copies[4].wait()
     w_copies[5].wait()
@@ -148,7 +159,7 @@
     w_copies[0].wait()
     w_copies[1].wait()
 
-    def project(p, first_pair):
+    def project_kv(p):
         for i in range(2):
             x_copy(2 * p + i).wait()
         x_pair = x_s[pl.ds(2 * p, 2)].reshape(2 * tok, dim).astype(F32)
@@ -163,73 +174,86 @@
         for i in range(2):
             kv_s[2 * p + i, me, 0] = k_rot[:, i * tok:(i + 1) * tok].T
             kv_s[2 * p + i, me, 1] = v_t[:, i * tok:(i + 1) * tok]
-        if first_pair:
-            pl.semaphore_wait(barrier, n_cp - 1)
-
-        def start_own(j):
+        normed_s[p % 2] = normed
+        cos_s[p % 2] = cos
+        sin_s[p % 2] = sin
+
+    def start_own(p):
+        def start(j):
             for i in range(2):
                 @pl.when(2 * p + i < PACED[j])
                 def _():
                     own(j, 2 * p + i, lambda copy: copy.start())
                 send(2 * p + i, me, partner, S_PART).start()
-        on_chip(start_own)
-        if first_pair:
-            w_copies[2].wait()
-        q_t = tdot(wq_s[...], normed, ((0,), (1,)))
+        on_chip(start)
+
+    def project_q(p):
+        cos, sin = cos_s[p % 2], sin_s[p % 2]
+        q_t = tdot(wq_s[...], normed_s[p % 2], ((0,), (1,)))
         zeros = jnp.zeros((head, tok), BF16)
         for n in range(n_heads):
-            q_rot = rope(q_t[n * head:(n + 1) * head], cos, sin).astype(F32) * scale
-            high = q_rot.astype(BF16)
-            low = (q_rot - high.astype(F32)).astype(BF16)
+            q_rot = rope(q_t[n * head:(n + 1) * head], cos, sin)
             col = (n % 2) * tok
             for i in range(2):
-                for part, q_part in enumerate((high, low)):
-                    for g in range(n_kv):
-                        q_s[2 * p + i, n // 2, part, g * head:(g + 1) * head, col:col + tok] = (
-                            q_part[:, i * tok:(i + 1) * tok] if g == n // group else zeros)
-
-    project(0, True)
+                for g in range(n_kv):
+                    q_s[2 * p + i, n // 2, g * head:(g + 1) * head, col:col + tok] = (
+                        q_rot[:, i * tok:(i + 1) * tok] if g == n // group else zeros)
+
+    project_kv(0)
+    pl.semaphore_wait(barrier, n_cp - 1)
+    start_own(0)
+    w_copies[2].wait()
 
     @pl.loop(1, batch // 2)
     def _(p):
-        project(p, False)
-
+        project_kv(p)
+        project_q(p - 1)
+        start_own(p)
+
+    project_q(batch // 2 - 1)
     w_copies[3].wait()
 
-    def scores(b, t, c, chunks):
+    units = [(t, min(2, n_pairs - t)) for t in range(0, n_pairs, 2)]
+
+    def scores(b, u, c, chunks):
+        first_t, width = units[u]
         k_blk = jnp.concatenate([kv_s[b, 2 * c, 0], kv_s[b, 2 * c + 1, 0]], axis=0)
-        s_blk = tdot(jnp.concatenate([k_blk, k_blk], axis=1), q_s[b, t].reshape(2 * kv_dim, 2 * tok), ((1,), (0,)))
+        q_unit = jnp.concatenate([q_s[b, first_t + i] for i in range(width)], axis=1)
+        s_blk = tdot(k_blk, q_unit, ((1,), (0,)))
         if c == chunks - 1:
-            bias = bias_s[...]
-            s_blk = s_blk + jnp.concatenate([bias, bias], axis=1)
-        score_s[t % 2, 2 * tok * c:2 * tok * (c + 1)] = s_blk
+            s_blk = s_blk + jnp.concatenate([bias_s[...]] * (2 * width), axis=1)
+        score_s[u % 2, 2 * tok * c:2 * tok * (c + 1), :2 * tok * width] = s_blk
         return jnp.max(s_blk, axis=0, keepdims=True)
 
     def attend(b, chunks, between):
         top = functools.reduce(jnp.maximum, [scores(b, 0, c, chunks) for c in range(chunks)])
-        for t in range(n_pairs):
-            if t == SPLIT:
+        for u, (first_t, width) in enumerate(units):
+            if u == SPLIT:
                 between()
             probs, total, next_top = [], None, None
             for c in range(chunks):
-                if t + 1 < n_pairs:
-                    part = scores(b, t + 1, c, chunks)
+                if u + 1 < len(units):
+                    part = scores(b, u + 1, c, chunks)
                     next_top = part if c == 0 else jnp.maximum(next_top, part)
-                prob = jnp.exp2(score_s[t % 2, 2 * tok * c:2 * tok * (c + 1)] - top)
+                prob = jnp.exp2((score_s[u % 2, 2 * tok * c:2 * tok * (c + 1), :2 * tok * width] - top) * scale)
                 part = jnp.sum(prob, axis=0, keepdims=True)
                 total = part if c == 0 else total + part
                 probs.append(prob)
-            lo, hi = (2 * t) // group, (2 * t + 1) // group
-            v_rows = slice(lo * head, (hi + 1) * head)
-            v_blk = jnp.concatenate([kv_s[b, s, 1][v_rows] for s in range(2 * chunks)], axis=1)
-            out = tdot(v_blk, jnp.concatenate(probs, axis=0), ((1,), (0,)))
             inv = 1.0 / total
-            halves = []
-            for i in range(2):
-                row = ((2 * t + i) // group - lo) * head
-                cols = slice(i * tok, (i + 1) * tok)
-                halves.append(out[row:row + head, cols] * inv[:, cols])
-            o_s[:, 2 * t * head:2 * (t + 1) * head] = jnp.concatenate(halves, axis=0).T.astype(BF16)
+            for w in range(width):
+                t = first_t + w
+                lo, hi = (2 * t) // group, (2 * t + 1) // group
+                v_rows = slice(lo * head, (hi + 1) * head)
+                v_blk = jnp.concatenate([kv_s[b, s, 1][v_rows] for s in range(2 * chunks)], axis=1)
+                pair = slice(2 * tok * w, 2 * tok * (w + 1))
+                out = tdot(v_blk, jnp.concatenate([prob[:, pair] for prob in probs], axis=0), ((1,), (0,)))
+                out_inv = inv[:, pair]
+                halves = []
+                for i in range(2):
+                    row = ((2 * t + i) // group - lo) * head
+                    cols = slice(i * tok, (i + 1) * tok)
+                    halves.append(out[row:row + head, cols] * out_inv[:, cols])
+                o_s[:, 2 * t * head:2 * (t + 1) * head] = jnp.concatenate(halves, axis=0).T.astype(BF16)
             top = next_top
 
     def pass_on(j):
@@ -293,14 +317,17 @@
                 pltpu.VMEM(positions.shape, jnp.int32),
                 pltpu.VMEM(norm_gain.shape, BF16),
                 pltpu.VMEM((head // 2, 2 * tok), F32),
+                pltpu.VMEM((2, head // 2, 2 * tok), F32),
+                pltpu.VMEM((2, head // 2, 2 * tok), F32),
+                pltpu.VMEM((2, 2 * tok, dim), BF16),
                 pltpu.VMEM(hidden.shape, BF16),
                 pltpu.VMEM(w_query.shape, BF16),
                 pltpu.VMEM(w_key.shape, BF16),
                 pltpu.VMEM(w_value.shape, BF16),
                 pltpu.VMEM((n_heads * head, dim), BF16),
-                pltpu.VMEM((batch, n_heads // 2, 2, kv_dim, 2 * tok), BF16),
+                pltpu.VMEM((batch, n_heads // 2, kv_dim, 2 * tok), BF16),
                 pltpu.VMEM((batch, n_cp, 2, tok, kv_dim), BF16),
-                pltpu.VMEM((2, n_cp * tok, 2 * tok), F32),
+                pltpu.VMEM((2, n_cp * tok, 4 * tok), F32),
                 pltpu.VMEM((2 * tok, tok), F32),
                 pltpu.VMEM((tok, n_heads * head), BF16),
                 pltpu.SemaphoreType.DMA((batch,)),
@@ -309,7 +336,7 @@
                 pltpu.SemaphoreType.DMA((batch, n_cp)),
             ],
             compiler_params=pltpu.CompilerParams(
-                collective_id=0, has_side_effects=True, vmem_limit_bytes=32 * 1024 * 1024),
+                collective_id=0, has_side_effects=True, vmem_limit_bytes=40 * 1024 * 1024),
             cost_estimate=pl.CostEstimate(flops=flops, bytes_accessed=8_000_000, transcendentals=0),
         )(*[pltpu.with_memory_space_constraint(arg, pltpu.HBM) for arg in (
             hidden, positions, norm_gain, w_query, w_key, w_value, w_out.reshape(n_heads * head, dim))])

time: 40.1 us -> 37.2 us (0.928)
  the two profiles are of different devices: /device:TPU:117 before, /device:TPU:119 now
where the time goes in v3:
time: 37.2 us; the launch traced here: 37.1 us
  Pallas kernels  35.9 us (97%)
  local copies, waits for them, and re-layouts  1.23 us (3%)
    pallas_call x1, Pallas kernels, local_block(): pl.pallas_call(functools.partial(block_kernel, n_cp, head), name='attenti...  35.9 us
    unnamed x1, local copies, waits for them, and re-layouts  1.23 us

profile of v3, /device:TPU:119, one launch (start us, length us, event | category | flops | bytes accessed | tf_op | source)
XLA Modules:
  0.0 37.1 jit_solution(10364351127769604296)
XLA Ops:
  0.0 35.9 %attention_block.1 = bf16[8,128,896]{2,1,0:T(8,128)(2,1)S(1)} custom-call(bf16[8,128,896]{2,1,0:T(8,128)(2,1)} %x_hbm.1, s32[8,128]{1,0:T(8,128)} %pos_hbm.1, bf16[896]{0:T(1024)(128)(2,1)} %gain_hbm.1, bf16[896,896]{1,0:T(8,128)(2,1)} %wq_hbm.1, bf16[896,128]{1,0:T(8,128)(2,1)} %wk_hbm.1, bf16[896,128]{1,0:T(8,128)(2,1)} %wv_hbm.1, bf16[896,896]{1,0:T(8,128)(2,1)} %bitcast.1), custom_call_target="tpu_custom_call" | custom-call | flops 7516192768 | bytes 8000000 | tf_op jit(solution)/shard_map/attention_block/pallas_call | solution.py:310
  35.9 1.2 %copy.9 = bf16[8,128,896]{2,1,0:T(8,128)(2,1)} copy(bf16[8,128,896]{2,1,0:T(8,128)(2,1)S(1)} %attention_block.1) | data formatting | bytes 3670016
